TPU v7x, 32 devices: a whole 2x2x4 slice. The times are simulated.
32 devices in a mesh: gx: 8 (over z, x), gy: 4 (over y, core).
Axes of the slice: x: 2, y: 2, z: 4, core: 2. Of those that a mesh axis runs over, the one named last changes fastest.
Arguments:
- gap_load: float32 [8, 4, 384, 128], P('gx', 'gy'), may hold values from -6 to 6
- flexibility: bfloat16 [8, 4, 768, 768], P('gx', 'gy'), as said below
- schur_blocks: bfloat16 [8, 4, 768, 768], P('gx', 'gy'), as said below
- body_modes: float32 [8, 4, 3, 768], P('gx', 'gy'), may hold values from -6 to 6
- coarse_inverse: float32 [96, 96], P(('gx', 'gy')), as said below
- saved_search: float32 [8, 4, 16, 384], P('gx', 'gy'), may hold values from -6 to 6
- saved_images: float32 [8, 4, 16, 384], P('gx', 'gy'), may hold values from -0.0068359375 to 0.0068359375
- face_slots: int32 [8, 4, 4, 192], P('gx', 'gy'), may hold values from 0 to 767, as said below
- face_count: int32 [8, 4, 4], P('gx', 'gy'), may hold values from 0 to 192, as said below
- multiplicity: int32 [8, 4, 768], P('gx', 'gy'), may hold values from 1 to 3, as said below
Outputs:
- multipliers: float32 [8, 4, 384, 128], P('gx', 'gy')
- residual: float32 [8, 4, 384, 128], P('gx', 'gy')
Inputs may be any that keep to these rules, and one draw needn't show every extreme that they name: For k < face_count[a, b, d] the entries face_slots[a, b, d, k] are distinct slots of subdomain (a, b), except that faces that follow each other in the order up, right, down, left share one slot when both are not empty. Link k of the face between two neighbouring subdomains is entry k of both their lists (down of the upper one and up of the lower one, right of the left one and left of the right one). Entries with k >= face_count carry no meaning. face_count[a, b, 0] = face_count[a - 1, b, 1] and face_count[a, b, 2] = face_count[a, b - 1, 3]; faces on the grid's border have 0 links, inner faces between 96 and 192, and in every draw some face along each grid direction has exactly 192. multiplicity[a, b, i] is 1 plus the number of faces of (a, b) whose first face_count entries name slot i. `flexibility`: each block is symmetric. `schur_blocks`: each block is symmetric. `coarse_inverse`: Symmetric.
All inputs are finite; a program needn't handle non-finite values.
Results may differ from a plain program's by a relative error of at most 0.0015.
The roundings to bfloat16 on the way count: a program that leaves them out, or rounds other values in their place, can miss the bound.
Values sent between devices are 32-bit elements.
A program may use at most 64 MiB of HBM per device.

v0:
```python
import jax
import jax.numpy as jnp
from jax import lax
from jax.sharding import PartitionSpec as P

HIGHEST_MODE = lax.Precision.HIGHEST


def shifted(value, axis, steps):
    count = lax.axis_size(axis)
    initial, last = (max(0, -steps), min(count, count - steps))
    return lax.ppermute(value, axis, [(source, source + steps) for source in range(initial, last)])


def place_parts(
    down_values, right_values, from_above, from_left, slot_table, face_valid, slot_total
):
    load_cases = down_values.shape[1]
    signed_parts = (
        jnp.stack([-from_above, down_values, -from_left, right_values], axis=0)
        * face_valid[:, :, None]
    )
    empty = jnp.zeros((slot_total, load_cases), jnp.float32)
    return empty.at[slot_table.reshape(-1)].add(signed_parts.reshape(-1, load_cases))


def place_full(full_links, slot_table, face_valid, slot_total):
    return place_parts(
        full_links[1],
        full_links[3],
        full_links[0],
        full_links[2],
        slot_table,
        face_valid,
        slot_total,
    )


def gain_copies(link_values, face_width):
    down_values = link_values[:face_width]
    right_values = link_values[face_width:]
    upper_copy = shifted(down_values, "gx", 1)
    left_copy = shifted(right_values, "gy", 1)
    return jnp.stack([upper_copy, down_values, left_copy, right_values], axis=0)


def own_links(full_links):
    return jnp.concatenate([full_links[1], full_links[3]], axis=0)


def jumps_full(slot_values, slot_table, face_valid):
    face_width = slot_table.shape[1]
    picked = jnp.take(slot_values, slot_table.reshape(-1), axis=0).reshape(
        4, face_width, slot_values.shape[1]
    )
    below_values = shifted(picked[0], "gx", -1)
    right_values = shifted(picked[2], "gy", -1)
    above_values = shifted(picked[1], "gx", 1)
    left_values = shifted(picked[3], "gy", 1)
    down_part = (picked[1] - below_values) * face_valid[1][:, None]
    right_part = (picked[3] - right_values) * face_valid[3][:, None]
    upper_part = (above_values - picked[0]) * face_valid[0][:, None]
    left_part = (left_values - picked[2]) * face_valid[2][:, None]
    return jnp.stack([upper_part, down_part, left_part, right_part], axis=0)


def late_dots(energy_part, intersect_part):
    return lax.psum((energy_part, intersect_part), ("gx", "gy"))


def curvature_sum(curvature_part):
    return lax.psum(curvature_part, ("gx", "gy"))


def per_device(
    gap_load,
    flexibility,
    schur_blocks,
    body_modes,
    coarse_inverse,
    saved_search,
    saved_images,
    face_slots,
    face_count,
    multiplicity,
):
    local_flex = flexibility[0, 0]
    local_schur = schur_blocks[0, 0]
    rigid_modes = body_modes[0, 0]
    slot_table = face_slots[0, 0]
    face_width = slot_table.shape[1]
    slot_total = rigid_modes.shape[1]
    face_valid = (jnp.arange(face_width)[None, :] < face_count[0, 0][:, None]).astype(jnp.float32)
    link_valid = jnp.concatenate([face_valid[1], face_valid[3]], axis=0)
    weights = 1.0 / multiplicity[0, 0].astype(jnp.float32)
    residual = gap_load[0, 0] * link_valid[:, None]
    kept_search = saved_search[0, 0] * link_valid[None, :]
    kept_images = saved_images[0, 0] * link_valid[None, :]
    residual_full = gain_copies(residual, face_width)
    search_full_kept = gain_copies(kept_search.T, face_width)
    weighted = (
        weights[:, None] * place_full(residual_full, slot_table, face_valid, slot_total)
    ).astype(jnp.bfloat16)
    smoothed = jnp.dot(local_schur, weighted, preferred_element_type=jnp.float32)
    precond_full = jumps_full(weights[:, None] * smoothed, slot_table, face_valid)
    precond = own_links(precond_full)
    energy_part = jnp.sum(own_links(residual_full) * precond, axis=0)
    coarse_in = jnp.dot(
        rigid_modes,
        place_full(precond_full, slot_table, face_valid, slot_total),
        precision=HIGHEST_MODE,
    )
    coarse_out = jnp.dot(
        coarse_inverse,
        lax.all_gather(coarse_in, ("gx", "gy"), axis=0, tiled=True),
        precision=HIGHEST_MODE,
    )
    projected_full = precond_full - jumps_full(
        jnp.dot(rigid_modes.T, coarse_out, precision=HIGHEST_MODE), slot_table, face_valid
    )
    intersect_part = jnp.dot(kept_images, own_links(projected_full), precision=HIGHEST_MODE)
    energy, intersect = late_dots(energy_part, intersect_part)
    search_full = projected_full - jnp.einsum(
        "dfj,jc->dfc", search_full_kept, intersect, precision=HIGHEST_MODE
    )
    lifted = place_full(search_full, slot_table, face_valid, slot_total).astype(jnp.bfloat16)
    applied_full = jumps_full(
        jnp.dot(local_flex, lifted, preferred_element_type=jnp.float32), slot_table, face_valid
    )
    search = own_links(search_full)
    curvature = curvature_sum(jnp.sum(search * own_links(applied_full), axis=0))
    step_size = energy / curvature
    multipliers = step_size * search
    residual_full = residual_full - step_size * applied_full
    residual = own_links(residual_full)
    return (multipliers[None, None], residual[None, None])


def solution(mesh):
    in_specs = (
        P("gx", "gy", None, None),
        P("gx", "gy", None, None),
        P("gx", "gy", None, None),
        P("gx", "gy", None, None),
        P(("gx", "gy"), None),
        P("gx", "gy", None, None),
        P("gx", "gy", None, None),
        P("gx", "gy", None, None),
        P("gx", "gy", None),
        P("gx", "gy", None),
    )
    out_specs = (P("gx", "gy", None, None), P("gx", "gy", None, None))
    return jax.shard_map(
        per_device, mesh=mesh, in_specs=in_specs, out_specs=out_specs, check_vma=False
    )
```

profile of v0, /device:TPU:0, one launch (start us, length us, event | category | flops | bytes accessed | tf_op | source)
XLA Modules:
  0.0 208.8 jit_solution(3762289602416720215)
XLA Ops:
  2.7 2.4 %collective-permute-start.1 = (f32[192,128]{1,0:T(8,128)S(1)}, f32[192,128]{1,0:T(8,128)S(1)}, u32[]{:S(2)}, u32[]{:S(2)}) collective-permute-start(f32[192,128]{1,0:T(8,128)S(1)} %get-tuple-element.48), channel_id=1, source_target_pairs={{0,1},{1,2},{2,3},{4,5},{5,6},{6,7},{8,9},{9,10},{10,11},{12,13},{... | collective-permute-start | bytes 294920 | tf_op jit(solution)/shard_map/ppermute | solution.py:12
  5.1 4.2 %collective-permute-start = (f32[192,128]{1,0:T(8,128)S(1)}, f32[192,128]{1,0:T(8,128)S(1)}, u32[]{:S(2)}, u32[]{:S(2)}) collective-permute-start(f32[192,128]{1,0:T(8,128)S(1)} %get-tuple-element.45), channel_id=1, source_target_pairs={{0,4},{4,8},{8,12},{12,16},{16,20},{20,24},{24,28},{1,5},{5,9},{9,... | collective-permute-start | bytes 294920 | tf_op jit(solution)/shard_map/ppermute | solution.py:12
  12.5 6.8 %scatter_custom_fusion = f32[768,128]{1,0:T(8,128)S(1)} fusion(s32[768]{0:T(1024)S(1)} %fusion.40, f32[768,128]{1,0:T(8,128)S(1)} %bitcast_multiply_fusion.2, f32[]{:T(128)} %constant.2.clone.1), kind=kCustom, calls=%fused_computation.53 | custom fusion | flops 98304 | bytes 393220 | tf_op jit(solution)/shard_map/scatter-add | solution.py:24
  20.1 1.6 gather_fusion
  21.9 4.1 %collective-permute-start.4 = (f32[192,128]{1,0:T(8,128)S(1)}, f32[192,128]{1,0:T(8,128)S(1)}, u32[]{:S(2)}, u32[]{:S(2)}) collective-permute-start(f32[192,128]{1,0:T(8,128)S(1)} %get-tuple-element.41), channel_id=1, source_target_pairs={{0,4},{4,8},{8,12},{12,16},{16,20},{20,24},{24,28},{1,5},{5,9},{9,... | collective-permute-start | bytes 294920 | tf_op jit(solution)/shard_map/ppermute | solution.py:12
  26.1 2.1 %collective-permute-start.5 = (f32[192,128]{1,0:T(8,128)S(1)}, f32[192,128]{1,0:T(8,128)S(1)}, u32[]{:S(2)}, u32[]{:S(2)}) collective-permute-start(f32[192,128]{1,0:T(8,128)S(1)} %get-tuple-element.43), channel_id=1, source_target_pairs={{0,1},{1,2},{2,3},{4,5},{5,6},{6,7},{8,9},{9,10},{10,11},{12,13},{... | collective-permute-start | bytes 294920 | tf_op jit(solution)/shard_map/ppermute | solution.py:12
  28.2 1.3 collective-permute-start.2
  29.5 1.3 collective-permute-start.3
  30.9 4.8 %collective-permute-done.2 = f32[192,128]{1,0:T(8,128)S(1)} collective-permute-done((f32[192,128]{1,0:T(8,128)S(1)}, f32[192,128]{1,0:T(8,128)S(1)}, u32[]{:S(2)}, u32[]{:S(2)}) %collective-permute-start.2) | collective-permute-done | bytes 98336 | tf_op jit(solution)/shard_map/ppermute | solution.py:12
  36.1 6.8 %scatter_custom_fusion.1 = f32[768,128]{1,0:T(8,128)S(1)} fusion(s32[768]{0:T(1024)S(1)} %fusion.40, f32[768,128]{1,0:T(8,128)S(1)} %bitcast_multiply_fusion.1, f32[]{:T(128)} %constant.2.clone.1), kind=kCustom, calls=%fused_computation.51 | custom fusion | flops 98304 | bytes 393220 | tf_op jit(solution)/shard_map/scatter-add | solution.py:24
  43.2 41.9 %all-gather = f32[32,3,128]{2,1,0:T(4,128)S(1)} all-gather(f32[1,3,128]{2,1,0:T(4,128)S(1)} %convolution_bitcast_fusion.2), channel_id=1, replica_groups=mesh['gx'=8,'gy'=4] {'gx','gy'}, dimensions={0}, use_global_device_ids=true | all-gather | bytes 50688 | tf_op jit(solution)/shard_map/all_gather | solution.py:115
  86.1 1.6 gather_fusion.1
  87.9 1.3 collective-permute-start.6
  89.2 1.3 collective-permute-start.7
  90.5 1.3 collective-permute-start.9
  91.8 3.0 %collective-permute-start.8 = (f32[192,128]{1,0:T(8,128)S(1)}, f32[192,128]{1,0:T(8,128)S(1)}, u32[]{:S(2)}, u32[]{:S(2)}) collective-permute-start(f32[192,128]{1,0:T(8,128)S(1)} %get-tuple-element.35), channel_id=1, source_target_pairs={{0,1},{1,2},{2,3},{4,5},{5,6},{6,7},{8,9},{9,10},{10,11},{12,13},{... | collective-permute-start | bytes 294920 | tf_op jit(solution)/shard_map/ppermute | solution.py:12
  94.9 3.5 %collective-permute-start.11 = (f32[192,16]{0,1:T(8,128)S(1)}, f32[192,16]{0,1:T(8,128)S(1)}, u32[]{:S(2)}, u32[]{:S(2)}) collective-permute-start(f32[192,16]{0,1:T(8,128)S(1)} %get-tuple-element.52), channel_id=1, source_target_pairs={{0,1},{1,2},{2,3},{4,5},{5,6},{6,7},{8,9},{9,10},{10,11},{12,13},{... | collective-permute-start | bytes 36872 | tf_op jit(solution)/shard_map/ppermute | solution.py:12
  98.4 4.3 %collective-permute-start.10 = (f32[192,16]{0,1:T(8,128)S(1)}, f32[192,16]{0,1:T(8,128)S(1)}, u32[]{:S(2)}, u32[]{:S(2)}) collective-permute-start(f32[192,16]{0,1:T(8,128)S(1)} %get-tuple-element.49), channel_id=1, source_target_pairs={{0,4},{4,8},{8,12},{12,16},{16,20},{20,24},{24,28},{1,5},{5,9},{9,... | collective-permute-start | bytes 36872 | tf_op jit(solution)/shard_map/ppermute | solution.py:12
  103.2 37.1 %psum.22 = f32[16,128]{1,0:T(8,128)S(1)} all-reduce(f32[16,128]{1,0:T(8,128)S(1)} %fusion.10), channel_id=1, replica_groups=mesh['gx'=8,'gy'=4] {'gx','gy'}, use_global_device_ids=true, to_apply=%region_4.6 | all-reduce | flops 2048 | bytes 16384 | tf_op jit(solution)/shard_map/psum | solution.py:68
  142.1 7.0 %scatter_custom_fusion.2 = f32[768,128]{1,0:T(8,128)S(1)} fusion(s32[768]{0:T(1024)} %copy-done.22, f32[768,128]{1,0:T(8,128)S(1)} %bitcast_multiply_fusion, f32[]{:T(128)} %constant.2.clone.1), kind=kCustom, calls=%fused_computation.49 | custom fusion | flops 98304 | bytes 393728 | tf_op jit(solution)/shard_map/scatter-add | solution.py:24
  149.9 1.6 gather_fusion.2
  151.8 4.1 %collective-permute-start.14 = (f32[192,128]{1,0:T(8,128)S(1)}, f32[192,128]{1,0:T(8,128)S(1)}, u32[]{:S(2)}, u32[]{:S(2)}) collective-permute-start(f32[192,128]{1,0:T(8,128)S(1)} %get-tuple-element.15), channel_id=1, source_target_pairs={{0,4},{4,8},{8,12},{12,16},{16,20},{20,24},{24,28},{1,5},{5,9},{9,... | collective-permute-start | bytes 294920 | tf_op jit(solution)/shard_map/ppermute | solution.py:12
  158.5 3.0 %collective-permute-start.15 = (f32[192,128]{1,0:T(8,128)S(1)}, f32[192,128]{1,0:T(8,128)S(1)}, u32[]{:S(2)}, u32[]{:S(2)}) collective-permute-start(f32[192,128]{1,0:T(8,128)S(1)} %get-tuple-element.17), channel_id=1, source_target_pairs={{0,1},{1,2},{2,3},{4,5},{5,6},{6,7},{8,9},{9,10},{10,11},{12,13},{... | collective-permute-start | bytes 294920 | tf_op jit(solution)/shard_map/ppermute | solution.py:12
  162.8 44.5 %all-reduce = (f32[128]{0:T(128)S(1)}, f32[128]{0:T(128)S(1)}) all-reduce(f32[128]{0:T(128)S(1)} %fusion.9, f32[128]{0:T(128)S(1)} %fusion.14), channel_id=1, replica_groups=mesh['gx'=8,'gy'=4] {'gx','gy'}, use_global_device_ids=true, to_apply=%region_2.4 | all-reduce | flops 256 | bytes 2048 | tf_op jit(solution)/shard_map/psum | solution.py:68
  (118 shorter events, 16.4 us)
Async XLA Ops:
  1.5 101.2 %copy-start.12 = (f32[1,192]{1,0:T(1,128)}, f32[1,192]{1,0:T(1,128)S(1)}, u32[]{:S(2)}) copy-start(f32[1,192]{1,0:T(1,128)S(1)} %get-tuple-element.56) | copy-start | bytes 2308
  1.5 101.2 %copy-start.18 = (f32[1,192]{1,0:T(1,128)}, f32[1,192]{1,0:T(1,128)S(1)}, u32[]{:S(2)}) copy-start(f32[1,192]{1,0:T(1,128)S(1)} %get-tuple-element.53) | copy-start | bytes 2308
  1.5 101.2 %copy-start.20 = (f32[1,192]{1,0:T(1,128)}, f32[1,192]{1,0:T(1,128)S(1)}, u32[]{:S(2)}) copy-start(f32[1,192]{1,0:T(1,128)S(1)} %get-tuple-element.54) | copy-start | bytes 2308
  2.7 9.0 %collective-permute-start.1 = (f32[192,128]{1,0:T(8,128)S(1)}, f32[192,128]{1,0:T(8,128)S(1)}, u32[]{:S(2)}, u32[]{:S(2)}) collective-permute-start(f32[192,128]{1,0:T(8,128)S(1)} %get-tuple-element.48), channel_id=1, source_target_pairs={{0,1},{1,2},{2,3},{4,5},{5,6},{6,7},{8,9},{9,10},{10,11},{12,13},{... | collective-permute-start | bytes 294920 | tf_op jit(solution)/shard_map/ppermute | solution.py:12
  5.1 6.7 %collective-permute-start = (f32[192,128]{1,0:T(8,128)S(1)}, f32[192,128]{1,0:T(8,128)S(1)}, u32[]{:S(2)}, u32[]{:S(2)}) collective-permute-start(f32[192,128]{1,0:T(8,128)S(1)} %get-tuple-element.45), channel_id=1, source_target_pairs={{0,4},{4,8},{8,12},{12,16},{16,20},{20,24},{24,28},{1,5},{5,9},{9,... | collective-permute-start | bytes 294920 | tf_op jit(solution)/shard_map/ppermute | solution.py:12
  10.9 76.7 %copy-start.16 = (pred[768]{0:T(1024)(128)(4,1)}, pred[768]{0:T(1024)(128)(4,1)S(1)}, u32[]{:S(2)}) copy-start(pred[768]{0:T(1024)(128)(4,1)S(1)} %compare_and_fusion) | copy-start | bytes 2308
  21.9 8.9 %collective-permute-start.4 = (f32[192,128]{1,0:T(8,128)S(1)}, f32[192,128]{1,0:T(8,128)S(1)}, u32[]{:S(2)}, u32[]{:S(2)}) collective-permute-start(f32[192,128]{1,0:T(8,128)S(1)} %get-tuple-element.41), channel_id=1, source_target_pairs={{0,4},{4,8},{8,12},{12,16},{16,20},{20,24},{24,28},{1,5},{5,9},{9,... | collective-permute-start | bytes 294920 | tf_op jit(solution)/shard_map/ppermute | solution.py:12
  26.1 4.8 %collective-permute-start.5 = (f32[192,128]{1,0:T(8,128)S(1)}, f32[192,128]{1,0:T(8,128)S(1)}, u32[]{:S(2)}, u32[]{:S(2)}) collective-permute-start(f32[192,128]{1,0:T(8,128)S(1)} %get-tuple-element.43), channel_id=1, source_target_pairs={{0,1},{1,2},{2,3},{4,5},{5,6},{6,7},{8,9},{9,10},{10,11},{12,13},{... | collective-permute-start | bytes 294920 | tf_op jit(solution)/shard_map/ppermute | solution.py:12
  28.2 7.5 %collective-permute-start.2 = (f32[192,128]{1,0:T(8,128)S(1)}, f32[192,128]{1,0:T(8,128)S(1)}, u32[]{:S(2)}, u32[]{:S(2)}) collective-permute-start(f32[192,128]{1,0:T(8,128)S(1)} %get-tuple-element.44), channel_id=1, source_target_pairs={{4,0},{8,4},{12,8},{16,12},{20,16},{24,20},{28,24},{5,1},{9,5},{13... | collective-permute-start | bytes 294920 | tf_op jit(solution)/shard_map/ppermute | solution.py:12
  29.5 6.2 %collective-permute-start.3 = (f32[192,128]{1,0:T(8,128)S(1)}, f32[192,128]{1,0:T(8,128)S(1)}, u32[]{:S(2)}, u32[]{:S(2)}) collective-permute-start(f32[192,128]{1,0:T(8,128)S(1)} %get-tuple-element.42), channel_id=1, source_target_pairs={{1,0},{2,1},{3,2},{5,4},{6,5},{7,6},{9,8},{10,9},{11,10},{13,12},{... | collective-permute-start | bytes 294920 | tf_op jit(solution)/shard_map/ppermute | solution.py:12
  35.9 49.3 %copy-start.23 = (f32[3,96]{1,0:T(4,128)S(1)}, f32[3,96]{1,0:T(4,128)}, u32[]{:S(2)}) copy-start(f32[3,96]{1,0:T(4,128)} %param.16) | copy-start | bytes 3460
  87.9 10.5 %collective-permute-start.6 = (f32[192,128]{1,0:T(8,128)S(1)}, f32[192,128]{1,0:T(8,128)S(1)}, u32[]{:S(2)}, u32[]{:S(2)}) collective-permute-start(f32[192,128]{1,0:T(8,128)S(1)} %get-tuple-element.33), channel_id=1, source_target_pairs={{0,4},{4,8},{8,12},{12,16},{16,20},{20,24},{24,28},{1,5},{5,9},{9,... | collective-permute-start | bytes 294920 | tf_op jit(solution)/shard_map/ppermute | solution.py:12
  89.2 13.5 %collective-permute-start.7 = (f32[192,128]{1,0:T(8,128)S(1)}, f32[192,128]{1,0:T(8,128)S(1)}, u32[]{:S(2)}, u32[]{:S(2)}) collective-permute-start(f32[192,128]{1,0:T(8,128)S(1)} %get-tuple-element.36), channel_id=1, source_target_pairs={{4,0},{8,4},{12,8},{16,12},{20,16},{24,20},{28,24},{5,1},{9,5},{13... | collective-permute-start | bytes 294920 | tf_op jit(solution)/shard_map/ppermute | solution.py:12
  90.5 12.2 %collective-permute-start.9 = (f32[192,128]{1,0:T(8,128)S(1)}, f32[192,128]{1,0:T(8,128)S(1)}, u32[]{:S(2)}, u32[]{:S(2)}) collective-permute-start(f32[192,128]{1,0:T(8,128)S(1)} %get-tuple-element.34), channel_id=1, source_target_pairs={{1,0},{2,1},{3,2},{5,4},{6,5},{7,6},{9,8},{10,9},{11,10},{13,12},{... | collective-permute-start | bytes 294920 | tf_op jit(solution)/shard_map/ppermute | solution.py:12
  91.8 10.9 %collective-permute-start.8 = (f32[192,128]{1,0:T(8,128)S(1)}, f32[192,128]{1,0:T(8,128)S(1)}, u32[]{:S(2)}, u32[]{:S(2)}) collective-permute-start(f32[192,128]{1,0:T(8,128)S(1)} %get-tuple-element.35), channel_id=1, source_target_pairs={{0,1},{1,2},{2,3},{4,5},{5,6},{6,7},{8,9},{9,10},{10,11},{12,13},{... | collective-permute-start | bytes 294920 | tf_op jit(solution)/shard_map/ppermute | solution.py:12
  94.9 45.4 %collective-permute-start.11 = (f32[192,16]{0,1:T(8,128)S(1)}, f32[192,16]{0,1:T(8,128)S(1)}, u32[]{:S(2)}, u32[]{:S(2)}) collective-permute-start(f32[192,16]{0,1:T(8,128)S(1)} %get-tuple-element.52), channel_id=1, source_target_pairs={{0,1},{1,2},{2,3},{4,5},{5,6},{6,7},{8,9},{9,10},{10,11},{12,13},{... | collective-permute-start | bytes 36872 | tf_op jit(solution)/shard_map/ppermute | solution.py:12
  98.4 41.9 %collective-permute-start.10 = (f32[192,16]{0,1:T(8,128)S(1)}, f32[192,16]{0,1:T(8,128)S(1)}, u32[]{:S(2)}, u32[]{:S(2)}) collective-permute-start(f32[192,16]{0,1:T(8,128)S(1)} %get-tuple-element.49), channel_id=1, source_target_pairs={{0,4},{4,8},{8,12},{12,16},{16,20},{20,24},{24,28},{1,5},{5,9},{9,... | collective-permute-start | bytes 36872 | tf_op jit(solution)/shard_map/ppermute | solution.py:12
  151.8 55.6 %copy-start.4 = (f32[192,128]{1,0:T(8,128)S(1)}, f32[192,128]{1,0:T(8,128)}, u32[]{:S(2)}) copy-start(f32[192,128]{1,0:T(8,128)} %copy-done.3) | copy-start | bytes 294916
  151.8 55.6 %copy-start.6 = (f32[192,128]{1,0:T(8,128)S(1)}, f32[192,128]{1,0:T(8,128)}, u32[]{:S(2)}) copy-start(f32[192,128]{1,0:T(8,128)} %copy-done.5) | copy-start | bytes 294916
  151.8 9.9 %collective-permute-start.14 = (f32[192,128]{1,0:T(8,128)S(1)}, f32[192,128]{1,0:T(8,128)S(1)}, u32[]{:S(2)}, u32[]{:S(2)}) collective-permute-start(f32[192,128]{1,0:T(8,128)S(1)} %get-tuple-element.15), channel_id=1, source_target_pairs={{0,4},{4,8},{8,12},{12,16},{16,20},{20,24},{24,28},{1,5},{5,9},{9,... | collective-permute-start | bytes 294920 | tf_op jit(solution)/shard_map/ppermute | solution.py:12
  155.9 6.5 %collective-permute-start.12 = (f32[192,128]{1,0:T(8,128)S(1)}, f32[192,128]{1,0:T(8,128)S(1)}, u32[]{:S(2)}, u32[]{:S(2)}) collective-permute-start(f32[192,128]{1,0:T(8,128)S(1)} %get-tuple-element.18), channel_id=1, source_target_pairs={{4,0},{8,4},{12,8},{16,12},{20,16},{24,20},{28,24},{5,1},{9,5},{13... | collective-permute-start | bytes 294920 | tf_op jit(solution)/shard_map/ppermute | solution.py:12
  157.2 5.2 %collective-permute-start.13 = (f32[192,128]{1,0:T(8,128)S(1)}, f32[192,128]{1,0:T(8,128)S(1)}, u32[]{:S(2)}, u32[]{:S(2)}) collective-permute-start(f32[192,128]{1,0:T(8,128)S(1)} %get-tuple-element.16), channel_id=1, source_target_pairs={{1,0},{2,1},{3,2},{5,4},{6,5},{7,6},{9,8},{10,9},{11,10},{13,12},{... | collective-permute-start | bytes 294920 | tf_op jit(solution)/shard_map/ppermute | solution.py:12
  158.5 4.0 %collective-permute-start.15 = (f32[192,128]{1,0:T(8,128)S(1)}, f32[192,128]{1,0:T(8,128)S(1)}, u32[]{:S(2)}, u32[]{:S(2)}) collective-permute-start(f32[192,128]{1,0:T(8,128)S(1)} %get-tuple-element.17), channel_id=1, source_target_pairs={{0,1},{1,2},{2,3},{4,5},{5,6},{6,7},{8,9},{9,10},{10,11},{12,13},{... | collective-permute-start | bytes 294920 | tf_op jit(solution)/shard_map/ppermute | solution.py:12
  162.7 44.8 %copy-start.7 = (f32[1,1,192,128]{3,2,1,0:T(8,128)S(1)}, f32[1,1,192,128]{3,2,1,0:T(8,128)}, u32[]{:S(2)}) copy-start(f32[1,1,192,128]{3,2,1,0:T(8,128)} %get-tuple-element.21) | copy-start | bytes 294916
  (16 other events, 184.6 us)
where the time goes:
time: 210 us; the launch traced here: 209 us
  blocking collectives  124 us (59%)
  starting transfers between devices  39.9 us (19%)
  other arithmetic  27.4 us (13%)
  local copies, waits for them, and re-layouts  7.75 us (4%)
  waiting for transfers between devices  5.63 us (3%)
  matrix products  3.22 us (2%)
    psum x2, blocking collectives, late_dots(): return lax.psum((energy_part, intersect_part), ('gx', 'gy'))  81.6 us
    all_gather x1, blocking collectives, per_device(): lax.all_gather(coarse_in, ('gx', 'gy'), axis=0, tiled=True)  41.9 us
    ppermute x16, starting transfers between devices, shifted(): lax.ppermute(value, axis, [(source, source + steps) for source in range(i...  39.9 us
    scatter-add x3, other arithmetic, place_parts(): empty.at[slot_table.reshape(-1)].add(signed_parts.reshape(-1, load_cases))  20.6 us
    ppermute x16, waiting for transfers between devices, shifted(): lax.ppermute(value, axis, [(source, source + steps) for source in range(i...  5.63 us
    gather x3, local copies, waits for them, and re-layouts, jumps_full(): jnp.take(slot_values, slot_table.reshape(-1), axis=0)  4.72 us
  transfers between devices with their start and end apart: 16, of which 2 were waited for; matrix products, arithmetic and copies ran while one was open for 1% of the time, Pallas kernels for 0%

commit v1 on v0

v1 whole, which is shorter than its diff:
```python
import functools

import jax
import jax.numpy as jnp
from jax import lax
from jax.experimental import pallas as pl
from jax.experimental.pallas import tpu as pltpu
from jax.sharding import PartitionSpec as P

HIGHEST_MODE = lax.Precision.HIGHEST
MESH = pl.DeviceIdType.MESH
F32 = jnp.float32
BF16 = jnp.bfloat16
FACE_ROWS = (1, 3, 0, 2)
MODE_ROWS = 8
SLOT_ROWS = 4


def split(value):
    high = value.astype(BF16)
    return high, (value - high.astype(F32)).astype(BF16)


def wide_dot(one_hot, value):
    width = value.shape[1]
    both = jnp.concatenate(split(value), axis=1)
    out = jnp.dot(one_hot, both, preferred_element_type=F32)
    return out[:, :width] + out[:, width:]


def fine_dot(left, right):
    rows, width = left.shape[0], right.shape[1]
    lefts = jnp.concatenate(split(left), axis=0)
    rights = jnp.concatenate(split(right), axis=1)
    out = jnp.dot(lefts, rights, preferred_element_type=F32)
    return (out[:rows, :width] + out[rows:, :width]) + (out[:rows, width:] + out[rows:, width:])


def kernel(
    nx, ny,
    gap_ref, flex_hbm, schur_hbm, modes_ref, inverse_ref, search_ref, images_ref, slots_ref,
    count_ref, mult_ref,
    out_mult, out_res,
    flex, schur, gather, scatter, weight_all, modes8, inverse8, modes_out, modes_in,
    inverse_pad, inverse_in, kept_out, kept_in, gap_in, parts, parts_in, coarse_out, coarse_in,
    all_coarse, sum_y, sum_x, dir_y, dir_x, all_curv, applied, applied_in,
    load_sem, face_send, face_recv, y_send, y_recv, x_send, x_recv, all_send, all_recv,
):
    n = nx * ny
    mx = lax.axis_index("gx")
    my = lax.axis_index("gy")
    me = mx * ny + my
    slot_total = mult_ref.shape[1]
    width = slots_ref.shape[1]
    cases = gap_ref.shape[1]
    ndir = search_ref.shape[0]
    links = 4 * width
    modes = modes_ref.shape[0]
    present = (mx < nx - 1, my < ny - 1, mx > 0, my > 0)
    beside = ((mx + 1, my), (mx, my + 1), (mx - 1, my), (mx, my - 1))

    def place(index):
        return (index // ny, lax.rem(index, ny))

    load_flex = pltpu.make_async_copy(flex_hbm, flex, load_sem.at[0])
    load_schur = pltpu.make_async_copy(schur_hbm, schur, load_sem.at[1])
    load_schur.start()
    load_flex.start()

    barrier = pltpu.get_barrier_semaphore()

    def greet(step, carry):
        pl.semaphore_signal(
            barrier, inc=1, device_id=place(lax.rem(me + step, n)), device_id_type=MESH
        )
        return carry

    lax.fori_loop(1, n, greet, 0)

    def face_copy(kind, src, dst_of, face, arriving):
        landing = face if arriving else (face + 2) % 4
        return pltpu.make_async_remote_copy(
            src_ref=src, dst_ref=dst_of(landing),
            send_sem=face_send.at[kind, face], recv_sem=face_recv.at[kind, landing],
            device_id=beside[face], device_id_type=MESH,
        )

    def send_face(kind, src, dst_of, face):
        @pl.when(present[face])
        def _():
            face_copy(kind, src, dst_of, face, False).start()

    def recv_face(kind, src, dst_of, face):
        @pl.when(present[face])
        def _():
            face_copy(kind, src, dst_of, face, True).wait_recv()

    def sent_face(kind, src, dst_of, face):
        @pl.when(present[face])
        def _():
            face_copy(kind, src, dst_of, face, False).wait_send()

    def row_of(face):
        row = slots_ref[FACE_ROWS[face] : FACE_ROWS[face] + 1, :]
        at = lax.broadcasted_iota(jnp.int32, (1, width), 1)
        return jnp.where(at < count_ref[0, FACE_ROWS[face]], row, -1).astype(F32)

    slot_row = jnp.concatenate([row_of(face) for face in range(4)], axis=1)
    slot_at = lax.broadcasted_iota(jnp.int32, (slot_total, links), 0).astype(F32)
    scatter[...] = jnp.where(slot_at == slot_row, 1.0, 0.0).astype(BF16)

    modes8[...] = jnp.zeros_like(modes8)
    modes8[0:modes, :] = modes_ref[...]
    mode_parts = jnp.concatenate(split(modes8[...]), axis=0)
    rest = modes8[...] - mode_parts[:MODE_ROWS].astype(F32) - mode_parts[MODE_ROWS:].astype(F32)
    mode_parts = jnp.concatenate(
        [mode_parts[:MODE_ROWS].astype(F32), mode_parts[MODE_ROWS:].astype(F32), rest], axis=0
    ).astype(BF16)
    picked3 = jnp.dot(mode_parts, scatter[...], preferred_element_type=F32)
    picked_modes = (
        picked3[:MODE_ROWS] + picked3[MODE_ROWS : 2 * MODE_ROWS] + picked3[2 * MODE_ROWS :]
    )
    for face in range(4):
        modes_out[face] = picked_modes[:, face * width : (face + 1) * width]

    inverse8[...] = jnp.zeros_like(inverse8)
    inverse8[0:modes, :] = inverse_ref[...]
    chunk = min(n, 32)
    from_at = lax.broadcasted_iota(jnp.int32, (modes * chunk, SLOT_ROWS * chunk), 0)
    to_at = lax.broadcasted_iota(jnp.int32, (modes * chunk, SLOT_ROWS * chunk), 1)
    inner = to_at % SLOT_ROWS
    expand = jnp.where((inner < modes) & (from_at == (to_at // SLOT_ROWS) * modes + inner), 1.0, 0.0)
    for at in range(n // chunk):
        inverse_pad[:, at * SLOT_ROWS * chunk : (at + 1) * SLOT_ROWS * chunk] = jnp.dot(
            inverse8[:, at * modes * chunk : (at + 1) * modes * chunk], expand,
            precision=HIGHEST_MODE, preferred_element_type=F32,
        )

    for face in range(2):
        kept_out[face, 0:ndir, :] = search_ref[:, face * width : (face + 1) * width]
        kept_out[face, ndir:, :] = images_ref[:, face * width : (face + 1) * width]

    pl.semaphore_wait(barrier, n - 1)

    def modes_dst(face):
        return modes_in.at[face]

    def inverse_dst(face):
        return inverse_in.at[face]

    def kept_dst(face):
        return kept_in.at[face - 2]

    def gap_dst(face):
        return gap_in.at[face - 2]

    for face in range(2):
        send_face(2, kept_out.at[face], kept_dst, face)
        send_face(0, modes_out.at[face], modes_dst, face)
        send_face(1, inverse_pad, inverse_dst, face)
        send_face(3, gap_ref.at[pl.ds(face * width, width)], gap_dst, face)
    for face in range(2, 4):
        send_face(0, modes_out.at[face], modes_dst, face)
        send_face(1, inverse_pad, inverse_dst, face)

    columns = jnp.transpose(jnp.broadcast_to(slot_row, (128, links)))
    lane = lax.broadcasted_iota(jnp.int32, (links, 128), 1).astype(F32)
    for at in range(slot_total // 128):
        gather[:, at * 128 : (at + 1) * 128] = jnp.where(
            columns == lane + float(at * 128), 1.0, 0.0
        ).astype(BF16)
    weight_row = 1.0 / mult_ref[...].astype(F32)
    weight_all[...] = jnp.transpose(jnp.broadcast_to(weight_row, (cases, slot_total)))

    row_at = lax.broadcasted_iota(jnp.int32, (width, cases), 0)

    def masked(value, face):
        return jnp.where(row_at < count_ref[0, FACE_ROWS[face]], value, 0.0)

    own_gap = jnp.concatenate(
        [masked(gap_ref[face * width : (face + 1) * width, :], face) for face in range(2)], axis=0
    )
    own_spread = wide_dot(scatter[:, : 2 * width], own_gap)

    for face in range(4):
        recv_face(0, modes_out.at[face], modes_dst, face)
        recv_face(1, inverse_pad, inverse_dst, face)
    for face in range(2, 4):
        recv_face(2, kept_out.at[face - 2], kept_dst, face)

    def lanes_masked(value, face):
        at = lax.broadcasted_iota(jnp.int32, value.shape, 1)
        return jnp.where(at < count_ref[0, FACE_ROWS[face]], value, 0.0)

    near = jnp.concatenate([lanes_masked(-modes_in[face], face) for face in range(4)], axis=1)
    at = lax.broadcasted_iota(jnp.int32, near.shape, 1)
    blocks = [picked_modes]
    for face in range(4):
        blocks.append(jnp.where((at >= face * width) & (at < (face + 1) * width), near, 0.0))
    mode_rows = jnp.concatenate(blocks, axis=0)
    kept = [lanes_masked(kept_out[face], face) for face in range(2)]
    kept += [lanes_masked(-kept_in[face - 2], face) for face in range(2, 4)]
    kept = jnp.concatenate(kept, axis=1)
    kept_search, kept_images = kept[:ndir], kept[ndir:]
    measure_rows = jnp.concatenate([mode_rows, kept_images], axis=0)
    filler = jnp.zeros((128 - 5 * MODE_ROWS - ndir, links), F32)
    lift = jnp.transpose(jnp.concatenate([mode_rows, kept_search, filler], axis=0))
    lift_high, lift_low = split(lift)
    lift3 = jnp.concatenate([lift_high, lift_high, lift_low], axis=1)

    own_part = lax.dot_general(
        kept_images, picked_modes, (((1,), (1,)), ((), ())),
        precision=HIGHEST_MODE, preferred_element_type=F32,
    )
    direct = jnp.dot(
        own_part, inverse_pad[...], precision=HIGHEST_MODE, preferred_element_type=F32
    )

    def y_copy(kind, buffer, step, arriving):
        slot = lax.rem(my - step + ny, ny) if arriving else my
        return pltpu.make_async_remote_copy(
            src_ref=buffer.at[my], dst_ref=buffer.at[slot],
            send_sem=y_send.at[kind, step], recv_sem=y_recv.at[kind, step],
            device_id=(mx, lax.rem(my + step, ny)), device_id_type=MESH,
        )

    def x_copy(kind, buffer, step, arriving):
        slot = lax.rem(mx - step + nx, nx) if arriving else mx
        return pltpu.make_async_remote_copy(
            src_ref=buffer.at[mx], dst_ref=buffer.at[slot],
            send_sem=x_send.at[kind, step], recv_sem=x_recv.at[kind, step],
            device_id=(lax.rem(mx + step, nx), my), device_id_type=MESH,
        )

    def all_copy(kind, buffer, step):
        return pltpu.make_async_remote_copy(
            src_ref=buffer.at[me], dst_ref=buffer.at[me],
            send_sem=all_send.at[kind], recv_sem=all_recv.at[kind],
            device_id=place(lax.rem(me + step, n)), device_id_type=MESH,
        )

    def every(kind, buffer):
        whole = buffer.at[pl.ds(0, n - 1)]
        return pltpu.make_async_remote_copy(
            src_ref=whole, dst_ref=whole,
            send_sem=all_send.at[kind], recv_sem=all_recv.at[kind],
            device_id=place(lax.rem(me + 1, n)), device_id_type=MESH,
        )

    def send_all(kind, buffer):
        def one(step, carry):
            all_copy(kind, buffer, step).start()
            return carry

        lax.fori_loop(1, n, one, 0)

    dir_y[my] = direct
    for step in range(1, ny):
        y_copy(0, dir_y, step, False).start()

    for face in range(2, 4):
        recv_face(3, gap_ref.at[pl.ds((face - 2) * width, width)], gap_dst, face)
    far_gap = jnp.concatenate([masked(-gap_in[face - 2], face) for face in range(2, 4)], axis=0)
    spread = own_spread + wide_dot(scatter[:, 2 * width :], far_gap)
    weighted = (weight_all[...] * spread).astype(BF16)
    load_schur.wait()
    smoothed = jnp.dot(schur[...], weighted, preferred_element_type=F32)
    picks = wide_dot(gather[...], weight_all[...] * smoothed)
    measured = fine_dot(measure_rows, picks)
    for face in range(4):
        coarse_out[face] = measured[(face + 1) * MODE_ROWS : (face + 2) * MODE_ROWS]
    sum_y[my] = measured[5 * MODE_ROWS :]

    def coarse_dst(face):
        return coarse_in.at[face]

    def parts_dst(face):
        return parts_in.at[face]

    for face in range(4):
        send_face(4, coarse_out.at[face], coarse_dst, face)
    for step in range(1, ny):
        y_copy(1, sum_y, step, False).start()
    for face in range(4):
        parts[face] = picks[face * width : (face + 1) * width]
    for face in range(4):
        send_face(5, parts.at[face], parts_dst, face)

    energy_part = jnp.sum(own_gap * picks[: 2 * width], axis=0, keepdims=True) + jnp.sum(
        far_gap * picks[2 * width :], axis=0, keepdims=True
    )

    for face in range(4):
        recv_face(4, coarse_out.at[face], coarse_dst, face)
    coarse = measured[:MODE_ROWS]
    for face in range(4):
        coarse = coarse + jnp.where(present[face], coarse_in[face], 0.0)
    mode_at = lax.broadcasted_iota(jnp.int32, (SLOT_ROWS, cases), 0)
    all_coarse[me] = jnp.where(mode_at < modes, coarse[:SLOT_ROWS], energy_part)
    send_all(0, all_coarse)

    for kind, from_y, to_x in ((1, sum_y, sum_x), (0, dir_y, dir_x)):
        for step in range(1, ny):
            y_copy(kind, from_y, step, True).wait_recv()
        to_x[mx] = jnp.sum(from_y[...], axis=0)
        for step in range(1, nx):
            x_copy(kind, to_x, step, False).start()

    for face in range(4):
        recv_face(5, parts.at[face], parts_dst, face)
    opened = picks - jnp.concatenate([masked(parts_in[face], face) for face in range(4)], axis=0)

    for kind, to_x in ((0, dir_x), (1, sum_x)):
        for step in range(1, nx):
            x_copy(kind, to_x, step, True).wait_recv()
    coarse_rows = [inverse_pad[...]]
    coarse_rows += [jnp.where(present[face], inverse_in[face], 0.0) for face in range(4)]
    coarse_rows.append(jnp.sum(dir_x[...], axis=0))
    coarse_rows = jnp.concatenate(coarse_rows, axis=0)
    direct_sum = jnp.sum(sum_x[...], axis=0)
    every(0, all_coarse).wait_recv()
    gathered = all_coarse[...]
    energy = jnp.sum(gathered, axis=0)[modes : modes + 1]
    solved = fine_dot(coarse_rows, gathered.reshape(SLOT_ROWS * n, cases))
    factors = jnp.concatenate(
        [
            solved[: 5 * MODE_ROWS],
            direct_sum - solved[5 * MODE_ROWS :],
            jnp.zeros((128 - 5 * MODE_ROWS - ndir, cases), F32),
        ],
        axis=0,
    )
    high, low = split(factors)
    search = opened - jnp.dot(
        lift3, jnp.concatenate([high, low, high], axis=0), preferred_element_type=F32
    )

    lifted = wide_dot(scatter[...], search).astype(BF16)
    load_flex.wait()
    bent = jnp.dot(flex[...], lifted, preferred_element_type=F32)
    picks2 = wide_dot(gather[...], bent)
    all_curv[me] = jnp.sum(search * picks2, axis=0, keepdims=True)
    send_all(1, all_curv)
    for face in range(2):
        applied[face] = picks2[(face + 2) * width : (face + 3) * width]

    def applied_dst(face):
        return applied_in.at[face]

    for face in range(2, 4):
        send_face(6, applied.at[face - 2], applied_dst, face)
    for face in range(2):
        recv_face(6, applied.at[face], applied_dst, face)
    moved = picks2[: 2 * width] - jnp.concatenate(
        [masked(applied_in[face], face) for face in range(2)], axis=0
    )
    every(1, all_curv).wait_recv()
    curvature = jnp.sum(all_curv[...], axis=0)
    step_size = energy / curvature
    out_mult[...] = step_size * search[: 2 * width]
    out_res[...] = own_gap - step_size * moved

    for face in range(4):
        sent_face(0, modes_out.at[face], modes_dst, face)
        sent_face(1, inverse_pad, inverse_dst, face)
        sent_face(4, coarse_out.at[face], coarse_dst, face)
        sent_face(5, parts.at[face], parts_dst, face)
    for face in range(2):
        sent_face(2, kept_out.at[face], kept_dst, face)
        sent_face(3, gap_ref.at[pl.ds(face * width, width)], gap_dst, face)
    for face in range(2, 4):
        sent_face(6, applied.at[face - 2], applied_dst, face)
    for kind, y_buffer, x_buffer in ((0, dir_y, dir_x), (1, sum_y, sum_x)):
        for step in range(1, ny):
            y_copy(kind, y_buffer, step, False).wait_send()
        for step in range(1, nx):
            x_copy(kind, x_buffer, step, False).wait_send()
    every(0, all_coarse).wait_send()
    every(1, all_curv).wait_send()


def per_device(
    nx, ny, gap_load, flexibility, schur_blocks, body_modes, coarse_inverse, saved_search,
    saved_images, face_slots, face_count, multiplicity,
):
    n = nx * ny
    links2, cases = gap_load.shape[2:]
    width = links2 // 2
    modes, slot_total = body_modes.shape[2:]
    ndir = saved_search.shape[2]
    padded = SLOT_ROWS * n
    vmem = pl.BlockSpec(memory_space=pltpu.VMEM)
    hbm = pl.BlockSpec(memory_space=pl.ANY)
    smem = pl.BlockSpec(memory_space=pltpu.SMEM)
    dma = pltpu.SemaphoreType.DMA
    scratch = [
        pltpu.VMEM((slot_total, slot_total), BF16),
        pltpu.VMEM((slot_total, slot_total), BF16),
        pltpu.VMEM((4 * width, slot_total), BF16),
        pltpu.VMEM((slot_total, 4 * width), BF16),
        pltpu.VMEM((slot_total, cases), F32),
        pltpu.VMEM((MODE_ROWS, slot_total), F32),
        pltpu.VMEM((MODE_ROWS, modes * n), F32),
        pltpu.VMEM((4, MODE_ROWS, width), F32),
        pltpu.VMEM((4, MODE_ROWS, width), F32),
        pltpu.VMEM((MODE_ROWS, padded), F32),
        pltpu.VMEM((4, MODE_ROWS, padded), F32),
        pltpu.VMEM((2, 2 * ndir, width), F32),
        pltpu.VMEM((2, 2 * ndir, width), F32),
        pltpu.VMEM((2, width, cases), F32),
        pltpu.VMEM((4, width, cases), F32),
        pltpu.VMEM((4, width, cases), F32),
        pltpu.VMEM((4, MODE_ROWS, cases), F32),
        pltpu.VMEM((4, MODE_ROWS, cases), F32),
        pltpu.VMEM((n, SLOT_ROWS, cases), F32),
        pltpu.VMEM((ny, ndir, cases), F32),
        pltpu.VMEM((nx, ndir, cases), F32),
        pltpu.VMEM((ny, ndir, padded), F32),
        pltpu.VMEM((nx, ndir, padded), F32),
        pltpu.VMEM((n, 1, cases), F32),
        pltpu.VMEM((2, width, cases), F32),
        pltpu.VMEM((2, width, cases), F32),
        dma((2,)),
        dma((7, 4)),
        dma((7, 4)),
        dma((2, ny)),
        dma((2, ny)),
        dma((2, nx)),
        dma((2, nx)),
        dma((2,)),
        dma((2,)),
    ]
    out = jax.ShapeDtypeStruct((links2, cases), F32)
    multipliers, residual = pl.pallas_call(
        functools.partial(kernel, nx, ny),
        out_shape=(out, out),
        in_specs=[vmem, hbm, hbm, vmem, vmem, vmem, vmem, vmem, smem, vmem],
        out_specs=(vmem, vmem),
        scratch_shapes=scratch,
        compiler_params=pltpu.CompilerParams(
            collective_id=0, has_side_effects=True, vmem_limit_bytes=48 * 1024 * 1024
        ),
    )(
        gap_load[0, 0], flexibility[0, 0], schur_blocks[0, 0], body_modes[0, 0], coarse_inverse,
        saved_search[0, 0], saved_images[0, 0], face_slots[0, 0], face_count[0], multiplicity[0],
    )
    return (multipliers[None, None], residual[None, None])


def solution(mesh):
    in_specs = (
        P("gx", "gy", None, None),
        P("gx", "gy", None, None),
        P("gx", "gy", None, None),
        P("gx", "gy", None, None),
        P(("gx", "gy"), None),
        P("gx", "gy", None, None),
        P("gx", "gy", None, None),
        P("gx", "gy", None, None),
        P("gx", "gy", None),
        P("gx", "gy", None),
    )
    out_specs = (P("gx", "gy", None, None), P("gx", "gy", None, None))
    return jax.shard_map(
        functools.partial(per_device, mesh.shape["gx"], mesh.shape["gy"]),
        mesh=mesh, in_specs=in_specs, out_specs=out_specs, check_vma=False,
    )
```

time: 210 us -> 43.4 us (0.21)
  blocking collectives: 124 us -> 0 us
  starting transfers between devices: 39.9 us -> 0 us
  Pallas kernels: 0 us -> 32.5 us
  other arithmetic: 27.4 us -> 0 us
  waiting for transfers between devices: 5.63 us -> 0 us
  matrix products: 3.22 us -> 0 us
    psum x2 -> x0, blocking collectives: 81.6 us -> none  [late_dots(): return lax.psum((energy_part, intersect_part), ('gx', 'gy'))]
    all_gather x1 -> x0, blocking collectives: 41.9 us -> none  [per_device(): lax.all_gather(coarse_in, ('gx', 'gy'), axis=0, tiled=True)]
    ppermute x16 -> x0, starting transfers between devices: 39.9 us -> none  [shifted(): lax.ppermute(value, axis, [(source, source + steps) for source in range(i...]
    pallas_call x0 -> x1, Pallas kernels: none -> 32.5 us  [per_device(): pl.pallas_call(functools.partial(kernel, nx, ny), out_shape=(out, out), i...]
    scatter-add x3 -> x0, other arithmetic: 20.6 us -> none  [place_parts(): empty.at[slot_table.reshape(-1)].add(signed_parts.reshape(-1, load_cases))]
    unnamed x49 -> x21, local copies, waits for them, and re-layouts: 0.72 us -> 9.71 us
    ppermute x16 -> x0, waiting for transfers between devices: 5.63 us -> none  [shifted(): lax.ppermute(value, axis, [(source, source + steps) for source in range(i...]
    gather x3 -> x0, local copies, waits for them, and re-layouts: 4.72 us -> none  [jumps_full(): jnp.take(slot_values, slot_table.reshape(-1), axis=0)]
  transfers between devices with their start and end apart: 16 -> 0, of which waited for: 2 -> 0; matrix products, arithmetic and copies ran while one was open for 1% -> 0% of each run, Pallas kernels for 0% -> 0%
where the time goes in v1:
time: 43.4 us; the launch traced here: 42.9 us
  Pallas kernels  32.5 us (75%)
  local copies, waits for them, and re-layouts  9.71 us (22%)
  between operations  0.65 us (1%)
    pallas_call x1, Pallas kernels, per_device(): pl.pallas_call(functools.partial(kernel, nx, ny), out_shape=(out, out), i...  32.5 us
    unnamed x21, local copies, waits for them, and re-layouts  9.71 us

profile of v1, /device:TPU:0, one launch (start us, length us, event | category | flops | bytes accessed | tf_op | source)
XLA Modules:
  0.0 42.9 jit_solution(17948951021754775255)
XLA Ops:
  0.6 0.7 %copy.14 = f32[1,1,3,768]{3,2,1,0:T(4,128)S(1)} copy(f32[1,1,3,768]{3,1,2,0:T(1,128)} %param.13) | data formatting | bytes 18432
  1.3 0.0 copy-start
  1.3 1.3 %copy-done = bf16[1,1,768,768]{3,2,1,0:T(8,128)(2,1)S(1)} copy-done((bf16[1,1,768,768]{3,2,1,0:T(8,128)(2,1)S(1)}, bf16[1,1,768,768]{3,2,1,0:T(8,128)(2,1)}, u32[]{:S(2)}) %copy-start) | copy-done | bytes 1179672
  2.6 0.0 copy-start.1
  2.6 1.3 %copy-done.1 = bf16[1,1,768,768]{3,2,1,0:T(8,128)(2,1)S(1)} copy-done((bf16[1,1,768,768]{3,2,1,0:T(8,128)(2,1)S(1)}, bf16[1,1,768,768]{3,2,1,0:T(8,128)(2,1)}, u32[]{:S(2)}) %copy-start.1) | copy-done | bytes 1179672
  3.9 0.0 copy-start.2
  3.9 0.9 %copy-done.2 = f32[1,1,384,128]{3,2,1,0:T(8,128)S(1)} copy-done((f32[1,1,384,128]{3,2,1,0:T(8,128)S(1)}, f32[1,1,384,128]{3,2,1,0:T(8,128)}, u32[]{:S(2)}) %copy-start.2) | copy-done | bytes 196632
  4.8 0.0 copy-start.3
  4.8 0.7 %copy-done.3 = f32[1,1,16,384]{3,2,1,0:T(8,128)S(1)} copy-done((f32[1,1,16,384]{3,2,1,0:T(8,128)S(1)}, f32[1,1,16,384]{3,2,1,0:T(8,128)}, u32[]{:S(2)}) %copy-start.3) | copy-done | bytes 24600
  5.5 0.0 copy-start.4
  5.5 0.7 %copy-done.4 = f32[1,1,16,384]{3,2,1,0:T(8,128)S(1)} copy-done((f32[1,1,16,384]{3,2,1,0:T(8,128)S(1)}, f32[1,1,16,384]{3,2,1,0:T(8,128)}, u32[]{:S(2)}) %copy-start.4) | copy-done | bytes 24600
  6.3 0.0 copy-start.5
  6.3 0.7 %copy-done.5 = s32[1,1,4,192]{3,2,1,0:T(4,128)S(1)} copy-done((s32[1,1,4,192]{3,2,1,0:T(4,128)S(1)}, s32[1,1,4,192]{3,2,1,0:T(4,128)}, u32[]{:S(2)}) %copy-start.5) | copy-done | bytes 3096
  7.0 0.0 copy-start.6
  7.0 0.7 %copy-done.6 = s32[1,1,768]{2,1,0:T(1,128)S(1)} copy-done((s32[1,1,768]{2,1,0:T(1,128)S(1)}, s32[1,1,768]{2,1,0:T(1,128)}, u32[]{:S(2)}) %copy-start.6) | copy-done | bytes 3096
  7.7 0.0 copy-start.7
  7.7 0.7 %copy-done.7 = f32[3,96]{1,0:T(4,128)S(1)} copy-done((f32[3,96]{1,0:T(4,128)S(1)}, f32[3,96]{1,0:T(4,128)}, u32[]{:S(2)}) %copy-start.7) | copy-done | bytes 1176
  8.3 0.0 copy-start.8
  8.3 0.7 %copy-done.8 = s32[1,1,4]{2,1,0:T(1,128)S(1)} copy-done((s32[1,1,4]{2,1,0:T(1,128)S(1)}, s32[1,1,4]{2,1,0:T(1,128)}, u32[]{:S(2)}) %copy-start.8) | copy-done | bytes 40
  9.0 32.5 %shard_map.113 = (f32[384,128]{1,0:T(8,128)S(1)}, f32[384,128]{1,0:T(8,128)S(1)}) custom-call(f32[384,128]{1,0:T(8,128)S(1)} %bitcast.17, bf16[768,768]{1,0:T(8,128)(2,1)S(1)} %bitcast.13, bf16[768,768]{1,0:T(8,128)(2,1)S(1)} %bitcast.14, f32[3,768]{1,0:T(4,128)S(1)} %bitcast.18, f32[3,96]{1,0:T(4,128)S(1)} %copy-done.7, f32[16,384]{1,0:T(8,128)S(1)} %bitcast.19, ...), custom_call_target="tpu_custom_call" | custom-call | tf_op jit(solution)/shard_map/pallas_call | solution.py:434
  41.5 0.7 %copy.17 = f32[1,1,384,128]{3,2,1,0:T(8,128)} copy(f32[1,1,384,128]{3,2,1,0:T(8,128)S(1)} %bitcast.16) | data formatting | bytes 393216
  42.2 0.7 %copy.18 = f32[1,1,384,128]{3,2,1,0:T(8,128)} copy(f32[1,1,384,128]{3,2,1,0:T(8,128)S(1)} %bitcast.15) | data formatting | bytes 393216
Async XLA Ops:
  1.3 1.3 %copy-start = (bf16[1,1,768,768]{3,2,1,0:T(8,128)(2,1)S(1)}, bf16[1,1,768,768]{3,2,1,0:T(8,128)(2,1)}, u32[]{:S(2)}) copy-start(bf16[1,1,768,768]{3,2,1,0:T(8,128)(2,1)} %param.11) | copy-start | bytes 3538948
  2.6 1.3 %copy-start.1 = (bf16[1,1,768,768]{3,2,1,0:T(8,128)(2,1)S(1)}, bf16[1,1,768,768]{3,2,1,0:T(8,128)(2,1)}, u32[]{:S(2)}) copy-start(bf16[1,1,768,768]{3,2,1,0:T(8,128)(2,1)} %param.12) | copy-start | bytes 3538948
  3.9 0.9 %copy-start.2 = (f32[1,1,384,128]{3,2,1,0:T(8,128)S(1)}, f32[1,1,384,128]{3,2,1,0:T(8,128)}, u32[]{:S(2)}) copy-start(f32[1,1,384,128]{3,2,1,0:T(8,128)} %param.10) | copy-start | bytes 589828
  4.8 0.7 %copy-start.3 = (f32[1,1,16,384]{3,2,1,0:T(8,128)S(1)}, f32[1,1,16,384]{3,2,1,0:T(8,128)}, u32[]{:S(2)}) copy-start(f32[1,1,16,384]{3,2,1,0:T(8,128)} %param.15) | copy-start | bytes 73732
  5.5 0.7 %copy-start.4 = (f32[1,1,16,384]{3,2,1,0:T(8,128)S(1)}, f32[1,1,16,384]{3,2,1,0:T(8,128)}, u32[]{:S(2)}) copy-start(f32[1,1,16,384]{3,2,1,0:T(8,128)} %param.16) | copy-start | bytes 73732
  6.3 0.7 %copy-start.5 = (s32[1,1,4,192]{3,2,1,0:T(4,128)S(1)}, s32[1,1,4,192]{3,2,1,0:T(4,128)}, u32[]{:S(2)}) copy-start(s32[1,1,4,192]{3,2,1,0:T(4,128)} %param.17) | copy-start | bytes 9220
  7.0 0.7 %copy-start.6 = (s32[1,1,768]{2,1,0:T(1,128)S(1)}, s32[1,1,768]{2,1,0:T(1,128)}, u32[]{:S(2)}) copy-start(s32[1,1,768]{2,1,0:T(1,128)} %param.19) | copy-start | bytes 9220
  7.7 0.7 %copy-start.7 = (f32[3,96]{1,0:T(4,128)S(1)}, f32[3,96]{1,0:T(4,128)}, u32[]{:S(2)}) copy-start(f32[3,96]{1,0:T(4,128)} %inverse_ref.1) | copy-start | bytes 3460
  8.3 0.7 %copy-start.8 = (s32[1,1,4]{2,1,0:T(1,128)S(1)}, s32[1,1,4]{2,1,0:T(1,128)}, u32[]{:S(2)}) copy-start(s32[1,1,4]{2,1,0:T(1,128)} %param.18) | copy-start | bytes 52

commit v2 on v1

--- a/solution.py
+++ b/solution.py
@@ -28,6 +28,14 @@
     return out[:, :width] + out[:, width:]
 
 
+def full_dot(one_hot, value):
+    high, low = split(value)
+    last = ((value - high.astype(F32)) - low.astype(F32)).astype(BF16)
+    width = value.shape[1]
+    out = jnp.dot(one_hot, jnp.concatenate([high, low, last], axis=1), preferred_element_type=F32)
+    return out[:, :width] + (out[:, width : 2 * width] + out[:, 2 * width :])
+
+
 def fine_dot(left, right):
     rows, width = left.shape[0], right.shape[1]
     lefts = jnp.concatenate(split(left), axis=0)
@@ -38,9 +46,10 @@
 
 def kernel(
     nx, ny,
-    gap_ref, flex_hbm, schur_hbm, modes_ref, inverse_ref, search_ref, images_ref, slots_ref,
-    count_ref, mult_ref,
+    gap_hbm, flex_hbm, schur_hbm, modes_hbm, inverse_hbm, search_hbm, images_hbm, slots_hbm,
+    count_hbm, mult_hbm,
     out_mult, out_res,
+    gap_ref, modes_ref, inverse_ref, search_ref, images_ref, slots_ref, count_ref, mult_ref,
     flex, schur, gather, scatter, weight_all, modes8, inverse8, modes_out, modes_in,
     inverse_pad, inverse_in, kept_out, kept_in, gap_in, parts, parts_in, coarse_out, coarse_in,
     all_coarse, sum_y, sum_x, dir_y, dir_x, all_curv, applied, applied_in,
@@ -62,10 +71,19 @@
     def place(index):
         return (index // ny, lax.rem(index, ny))
 
-    load_flex = pltpu.make_async_copy(flex_hbm, flex, load_sem.at[0])
-    load_schur = pltpu.make_async_copy(schur_hbm, schur, load_sem.at[1])
-    load_schur.start()
-    load_flex.start()
+    loads = [
+        pltpu.make_async_copy(source, target, load_sem.at[at])
+        for at, (source, target) in enumerate(
+            (
+                (count_hbm, count_ref), (slots_hbm, slots_ref), (modes_hbm, modes_ref),
+                (inverse_hbm, inverse_ref), (search_hbm, search_ref), (images_hbm, images_ref),
+                (mult_hbm, mult_ref), (gap_hbm, gap_ref), (schur_hbm, schur), (flex_hbm, flex),
+            )
+        )
+    ]
+    for load in loads:
+        load.start()
+    load_schur, load_flex = loads[8:]
 
     barrier = pltpu.get_barrier_semaphore()
 
@@ -100,17 +118,24 @@
         def _():
             face_copy(kind, src, dst_of, face, False).wait_send()
 
+    for load in loads[:8]:
+        load.wait()
+
+    def count_of(face):
+        return count_ref[:, FACE_ROWS[face] : FACE_ROWS[face] + 1]
+
     def row_of(face):
         row = slots_ref[FACE_ROWS[face] : FACE_ROWS[face] + 1, :]
         at = lax.broadcasted_iota(jnp.int32, (1, width), 1)
-        return jnp.where(at < count_ref[0, FACE_ROWS[face]], row, -1).astype(F32)
+        return jnp.where(at < count_of(face), row, -1).astype(F32)
 
     slot_row = jnp.concatenate([row_of(face) for face in range(4)], axis=1)
     slot_at = lax.broadcasted_iota(jnp.int32, (slot_total, links), 0).astype(F32)
     scatter[...] = jnp.where(slot_at == slot_row, 1.0, 0.0).astype(BF16)
 
     modes8[...] = jnp.zeros_like(modes8)
-    modes8[0:modes, :] = modes_ref[...]
+    for mode in range(modes):
+        modes8[mode : mode + 1, :] = modes_ref[mode]
     mode_parts = jnp.concatenate(split(modes8[...]), axis=0)
     rest = modes8[...] - mode_parts[:MODE_ROWS].astype(F32) - mode_parts[MODE_ROWS:].astype(F32)
     mode_parts = jnp.concatenate(
@@ -175,12 +200,12 @@
     row_at = lax.broadcasted_iota(jnp.int32, (width, cases), 0)
 
     def masked(value, face):
-        return jnp.where(row_at < count_ref[0, FACE_ROWS[face]], value, 0.0)
+        return jnp.where(row_at < count_of(face), value, 0.0)
 
     own_gap = jnp.concatenate(
         [masked(gap_ref[face * width : (face + 1) * width, :], face) for face in range(2)], axis=0
     )
-    own_spread = wide_dot(scatter[:, : 2 * width], own_gap)
+    own_spread = full_dot(scatter[:, : 2 * width], own_gap)
 
     for face in range(4):
         recv_face(0, modes_out.at[face], modes_dst, face)
@@ -190,7 +215,7 @@
 
     def lanes_masked(value, face):
         at = lax.broadcasted_iota(jnp.int32, value.shape, 1)
-        return jnp.where(at < count_ref[0, FACE_ROWS[face]], value, 0.0)
+        return jnp.where(at < count_of(face), value, 0.0)
 
     near = jnp.concatenate([lanes_masked(-modes_in[face], face) for face in range(4)], axis=1)
     at = lax.broadcasted_iota(jnp.int32, near.shape, 1)
@@ -261,11 +286,11 @@
     for face in range(2, 4):
         recv_face(3, gap_ref.at[pl.ds((face - 2) * width, width)], gap_dst, face)
     far_gap = jnp.concatenate([masked(-gap_in[face - 2], face) for face in range(2, 4)], axis=0)
-    spread = own_spread + wide_dot(scatter[:, 2 * width :], far_gap)
+    spread = own_spread + full_dot(scatter[:, 2 * width :], far_gap)
     weighted = (weight_all[...] * spread).astype(BF16)
     load_schur.wait()
     smoothed = jnp.dot(schur[...], weighted, preferred_element_type=F32)
-    picks = wide_dot(gather[...], weight_all[...] * smoothed)
+    picks = full_dot(gather[...], weight_all[...] * smoothed)
     measured = fine_dot(measure_rows, picks)
     for face in range(4):
         coarse_out[face] = measured[(face + 1) * MODE_ROWS : (face + 2) * MODE_ROWS]
@@ -335,7 +360,7 @@
         lift3, jnp.concatenate([high, low, high], axis=0), preferred_element_type=F32
     )
 
-    lifted = wide_dot(scatter[...], search).astype(BF16)
+    lifted = full_dot(scatter[...], search).astype(BF16)
     load_flex.wait()
     bent = jnp.dot(flex[...], lifted, preferred_element_type=F32)
     picks2 = wide_dot(gather[...], bent)
@@ -391,9 +416,16 @@
     padded = SLOT_ROWS * n
     vmem = pl.BlockSpec(memory_space=pltpu.VMEM)
     hbm = pl.BlockSpec(memory_space=pl.ANY)
-    smem = pl.BlockSpec(memory_space=pltpu.SMEM)
     dma = pltpu.SemaphoreType.DMA
     scratch = [
+        pltpu.VMEM((links2, cases), F32),
+        pltpu.VMEM((modes, 1, slot_total), F32),
+        pltpu.VMEM((modes, modes * n), F32),
+        pltpu.VMEM((ndir, links2), F32),
+        pltpu.VMEM((ndir, links2), F32),
+        pltpu.VMEM((4, width), jnp.int32),
+        pltpu.VMEM((1, 4), jnp.int32),
+        pltpu.VMEM((1, slot_total), jnp.int32),
         pltpu.VMEM((slot_total, slot_total), BF16),
         pltpu.VMEM((slot_total, slot_total), BF16),
         pltpu.VMEM((4 * width, slot_total), BF16),
@@ -420,7 +452,7 @@
         pltpu.VMEM((n, 1, cases), F32),
         pltpu.VMEM((2, width, cases), F32),
         pltpu.VMEM((2, width, cases), F32),
-        dma((2,)),
+        dma((10,)),
         dma((7, 4)),
         dma((7, 4)),
         dma((2, ny)),
@@ -434,14 +466,14 @@
     multipliers, residual = pl.pallas_call(
         functools.partial(kernel, nx, ny),
         out_shape=(out, out),
-        in_specs=[vmem, hbm, hbm, vmem, vmem, vmem, vmem, vmem, smem, vmem],
+        in_specs=[hbm] * 10,
         out_specs=(vmem, vmem),
         scratch_shapes=scratch,
         compiler_params=pltpu.CompilerParams(
-            collective_id=0, has_side_effects=True, vmem_limit_bytes=48 * 1024 * 1024
+            collective_id=0, has_side_effects=True
         ),
     )(
-        gap_load[0, 0], flexibility[0, 0], schur_blocks[0, 0], body_modes[0, 0], coarse_inverse,
+        gap_load[0, 0], flexibility[0, 0], schur_blocks[0, 0], jnp.reshape(body_modes, (modes, 1, slot_total)), coarse_inverse,
         saved_search[0, 0], saved_images[0, 0], face_slots[0, 0], face_count[0], multiplicity[0],
     )
     return (multipliers[None, None], residual[None, None])

time: 43.4 us -> 37 us (0.85)
  local copies, waits for them, and re-layouts: 9.71 us -> 3.23 us
    unnamed x21 -> x2, local copies, waits for them, and re-layouts: 9.71 us -> 3.23 us
where the time goes in v2:
time: 37 us; the launch traced here: 36.8 us
  Pallas kernels  32.9 us (89%)
  local copies, waits for them, and re-layouts  3.23 us (9%)
  between operations  0.64 us (2%)
    pallas_call x1, Pallas kernels, per_device(): pl.pallas_call(functools.partial(kernel, nx, ny), out_shape=(out, out), i...  32.9 us
    unnamed x2, local copies, waits for them, and re-layouts  3.23 us

profile of v2, /device:TPU:0, one launch (start us, length us, event | category | flops | bytes accessed | tf_op | source)
XLA Modules:
  0.0 36.8 jit_solution(3709226927166082275)
XLA Ops:
  0.6 32.9 %shard_map.113 = (f32[384,128]{1,0:T(8,128)}, f32[384,128]{1,0:T(8,128)}) custom-call(f32[384,128]{1,0:T(8,128)} %bitcast.13, bf16[768,768]{1,0:T(8,128)(2,1)} %bitcast.11, bf16[768,768]{1,0:T(8,128)(2,1)} %bitcast.12, f32[3,1,768]{2,1,0:T(1,128)} %bitcast.18, f32[3,96]{1,0:T(4,128)} %inverse_hbm.1, f32[16,384]{1,0:T(8,128)} %bitcast.16, ...), custom_call_target="tpu_custom_call" | custom-call | tf_op jit(solution)/shard_map/pallas_call | solution.py:466
  33.5 1.6 %copy.14 = f32[1,1,384,128]{3,2,1,0:T(8,128)} copy(f32[1,1,384,128]{3,2,1,0:T(8,128)} %bitcast.15) | data formatting | bytes 393216
  35.2 1.6 %copy.15 = f32[1,1,384,128]{3,2,1,0:T(8,128)} copy(f32[1,1,384,128]{3,2,1,0:T(8,128)} %bitcast.14) | data formatting | bytes 393216
